TPU v7x, 128 devices: a whole 4x4x4 slice. The times are simulated.
128 devices in a mesh: rep: 1, data: 128 (over z, y, x, core).
Axes of the slice: x: 4, y: 4, z: 4, core: 2. Of those that a mesh axis runs over, the one named last changes fastest.
Arguments:
- hidden: bfloat16 [32768, 3072], P(('rep', 'data'))
- adapter_id: int32 [32768], P(('rep', 'data'))
- w_gate: bfloat16 [3072, 8192], replicated
- w_up: bfloat16 [3072, 8192], replicated
- w_down: bfloat16 [8192, 3072], replicated
- a_gate: bfloat16 [256, 3072, 8], replicated
- b_gate: bfloat16 [256, 8, 8192], P('data')
- a_up: bfloat16 [256, 3072, 8], replicated
- b_up: bfloat16 [256, 8, 8192], P('data')
- a_down: bfloat16 [256, 8192, 8], replicated
- b_down: bfloat16 [256, 8, 3072], P('data')
Outputs:
- output: bfloat16 [32768, 3072], P(('rep', 'data'))
All inputs are finite; a program needn't handle non-finite values.
Results may differ from a plain program's by a relative error of at most 0.00618975.
Values are sent between devices in bfloat16 or wider.
A program may use at most 1 GiB of HBM per device.

v0:
```python
import jax
import jax.numpy as jnp
from jax import lax
from jax.sharding import PartitionSpec as P

value_a10 = 2.0


def pick_low(act_rows, a_all, adapter_hot):
    all_low = jnp.einsum('tk,akr->tar', act_rows, a_all, preferred_element_type=jnp.float32)
    return jnp.sum(all_low * adapter_hot[:, :, None], axis=1).astype(jnp.bfloat16)


def value_a7(low_rows, local_hot, b_local):
    spread = local_hot[:, :, None] * low_rows[:, None, :]
    delta_out = jnp.einsum('mar,arf->mf', spread, b_local, preferred_element_type=jnp.float32)
    return (value_a10 * delta_out).astype(jnp.bfloat16)


def solution(mesh):
    groups = mesh.shape['data']
    row_spec = P(('rep', 'data'), None)
    tok_spec = P(('rep', 'data'))
    full_two = P(None, None)
    full_three = P(None, None, None)
    owned = P('data', None, None)

    def device_fn(hidden, adapter_id, w_gate, w_up, w_down, a_gate, b_gate, a_up, b_up, a_down, b_down):
        tok_local = hidden.shape[0]
        adapters = a_gate.shape[0]
        per_owner = b_gate.shape[0]
        value_a9 = a_gate.shape[2]
        capacity = min(4 * tok_local // groups, tok_local // 2)
        owner_ids = adapter_id // per_owner
        owner_hot = (owner_ids[:, None] == jnp.arange(groups)[None, :]).astype(jnp.int32)
        slot_rank = jnp.sum(jnp.cumsum(owner_hot, axis=0) * owner_hot, axis=1) - 1
        flat_slot = owner_ids * capacity + slot_rank
        adapter_hot = (adapter_id[:, None] == jnp.arange(adapters)[None, :]).astype(jnp.float32)

        send_ids = jnp.full((groups * capacity,), -1, jnp.int32).at[flat_slot].set(adapter_id % per_owner)
        recv_ids = lax.all_to_all(send_ids, 'data', 0, 0, tiled=True)
        local_hot = (recv_ids[:, None] == jnp.arange(per_owner)[None, :]).astype(jnp.bfloat16)

        low_both = jnp.concatenate([pick_low(hidden, a_gate, adapter_hot), pick_low(hidden, a_up, adapter_hot)], axis=1)
        send_low = jnp.zeros((groups * capacity, 2 * value_a9), jnp.bfloat16).at[flat_slot].set(low_both)
        recv_low = lax.all_to_all(send_low, 'data', 0, 0, tiled=True)
        delta_gate = value_a7(recv_low[:, :value_a9], local_hot, b_gate)
        delta_up = value_a7(recv_low[:, value_a9:], local_hot, b_up)
        back_gate = lax.all_to_all(delta_gate, 'data', 0, 0, tiled=True)
        back_up = lax.all_to_all(delta_up, 'data', 0, 0, tiled=True)

        gate_act = jnp.dot(hidden, w_gate, preferred_element_type=jnp.float32) + jnp.take(back_gate, flat_slot, axis=0).astype(jnp.float32)
        up_act = jnp.dot(hidden, w_up, preferred_element_type=jnp.float32) + jnp.take(back_up, flat_slot, axis=0).astype(jnp.float32)
        hid_act = (jax.nn.silu(gate_act) * up_act).astype(jnp.bfloat16)

        send_down = jnp.zeros((groups * capacity, value_a9), jnp.bfloat16).at[flat_slot].set(pick_low(hid_act, a_down, adapter_hot))
        recv_down = lax.all_to_all(send_down, 'data', 0, 0, tiled=True)
        back_down = lax.all_to_all(value_a7(recv_down, local_hot, b_down), 'data', 0, 0, tiled=True)
        down_act = jnp.dot(hid_act, w_down, preferred_element_type=jnp.float32) + jnp.take(back_down, flat_slot, axis=0).astype(jnp.float32)
        return (hidden.astype(jnp.float32) + down_act).astype(jnp.bfloat16)

    return jax.shard_map(device_fn, mesh=mesh, in_specs=(row_spec, tok_spec, full_two, full_two, full_two, full_three, owned, full_three, owned, full_three, owned), out_specs=row_spec, check_vma=False)
```

profile of v0, /device:TPU:2, one launch (start us, length us, event | category | flops | bytes accessed | tf_op | source)
XLA Modules:
  0.0 872.6 jit_solution(15743621734587142776)
XLA Ops:
  0.0 0.7 and_select_fusion
  0.9 0.2 fusion.28
  1.2 0.2 fusion.29
  1.3 1.4 scatter_custom_fusion
  2.8 0.7 all_to_all.44
  3.5 10.5 %all-to-all-start = ((s32[128,8,1]{1,2,0:T(1,128)}), s32[128,8,1]{1,2,0:T(1,128)S(1)}, u32[]{:S(2)}, u32[]{:S(2)}) async-start(s32[128,8,1]{1,2,0:T(1,128)} %bitcast.4), calls=%async_computation | async-start | bytes 131072 | tf_op jit(solution)/shard_map/all_to_all | solution.py:41
  14.0 0.7 fusion.27
  14.7 19.9 %multiply_reduce_fusion.1 = bf16[256,8]{0,1:T(8,128)(2,1)S(1)} fusion(f32[256,256]{0,1:T(8,128)S(1)} %fusion.27, bf16[256,3072,8]{1,2,0:T(8,128)(2,1)} %param.20, bf16[256,3072]{1,0:T(8,128)(2,1)} %param.13), kind=kOutput, calls=%fused_computation.30 | convolution fusion | flops 3222272000 | bytes 14422016 | tf_op jit(solution)/shard_map/tk,akr->tar/dot_general | solution.py:10
  34.6 19.1 %multiply_reduce_fusion.2 = bf16[256,8]{0,1:T(8,128)(2,1)S(1)} fusion(f32[256,256]{0,1:T(8,128)S(1)} %fusion.27, bf16[256,3072,8]{1,2,0:T(8,128)(2,1)} %param.18, bf16[256,3072]{1,0:T(8,128)(2,1)S(1)} %copy-done.3), kind=kOutput, calls=%fused_computation.31 | convolution fusion | flops 3222272000 | bytes 14422016 | tf_op jit(solution)/shard_map/tk,akr->tar/dot_general | solution.py:10
  53.9 1.9 scatter_custom_fusion.1
  55.8 9.8 %all-to-all-start.1 = ((bf16[128,8,16]{2,1,0:T(8,128)(2,1)}), bf16[128,8,16]{2,1,0:T(8,128)(2,1)S(1)}, u32[]{:S(2)}, u32[]{:S(2)}) async-start(bf16[128,8,16]{2,1,0:T(8,128)(2,1)} %bitcast.6), calls=%async_computation.1 | async-start | bytes 524288 | tf_op jit(solution)/shard_map/all_to_all | solution.py:46
  65.5 0.6 broadcast.123
  66.1 0.8 reduce.3
  67.1 8.6 all-to-all-done.1
  75.9 8.1 fusion.4
  84.0 6.3 all-to-all-start.2
  90.4 8.2 fusion.5
  98.6 236.7 %all-to-all-done.2 = bf16[128,8,8192]{2,1,0:T(8,128)(2,1)} async-done(((bf16[128,8,8192]{2,1,0:T(8,128)(2,1)}), bf16[128,8,8192]{2,1,0:T(8,128)(2,1)}, u32[]{:S(2)}, u32[]{:S(2)}) %all-to-all-start.2) | async-done | bytes 16777248 | tf_op jit(solution)/shard_map/all_to_all | solution.py:49
  335.3 13.3 %all-to-all-start.3 = ((bf16[128,8,8192]{2,1,0:T(8,128)(2,1)}), bf16[128,8,8192]{2,1,0:T(8,128)(2,1)}, u32[]{:S(2)}, u32[]{:S(2)}) async-start(bf16[128,8,8192]{2,1,0:T(8,128)(2,1)} %fusion.5), calls=%async_computation.3 | async-start | bytes 33554432 | tf_op jit(solution)/shard_map/all_to_all | solution.py:50
  348.7 17.0 %gather_fusion.1 = bf16[256,8192]{1,0:T(8,128)(2,1)} fusion(bf16[1024,8192]{1,0:T(8,128)(2,1)} %bitcast.10, s32[1024]{0:T(1024)S(1)} %pad_clamp_fusion), kind=kCustom, calls=%fused_computation.clone | custom fusion | bytes 8389632 | tf_op jit(solution)/shard_map/jit(_take)/gather | solution.py:52
  365.6 227.5 %all-to-all-done.3 = bf16[128,8,8192]{2,1,0:T(8,128)(2,1)} async-done(((bf16[128,8,8192]{2,1,0:T(8,128)(2,1)}), bf16[128,8,8192]{2,1,0:T(8,128)(2,1)}, u32[]{:S(2)}, u32[]{:S(2)}) %all-to-all-start.3) | async-done | bytes 16777248 | tf_op jit(solution)/shard_map/all_to_all | solution.py:50
  593.1 17.1 %gather_fusion.2 = bf16[256,8192]{1,0:T(8,128)(2,1)} fusion(bf16[1024,8192]{1,0:T(8,128)(2,1)} %bitcast.13, s32[1024]{0:T(1024)S(1)} %pad_clamp_fusion), kind=kCustom, calls=%fused_computation.1.clone | custom fusion | bytes 8389632 | tf_op jit(solution)/shard_map/jit(_take)/gather | solution.py:53
  610.2 26.2 %convolution_add_fusion.1 = f32[256,8192]{1,0:T(8,128)} fusion(bf16[256,3072]{1,0:T(8,128)(2,1)S(1)} %copy-done.3, bf16[3072,8192]{1,0:T(8,128)(2,1)} %param.15, bf16[256,8192]{1,0:T(8,128)(2,1)} %gather_fusion.1, pred[256]{0:T(512)(128)(4,1)S(1)} %get-tuple-element.6), kind=kOutput, calls=%fused_computation.22 | convolution fusion | flops 12891193344 | bytes 64487680 | tf_op jit(solution)/shard_map/dot_general | solution.py:52
  636.5 25.5 %fusion.12 = bf16[256,8192]{1,0:T(8,128)(2,1)} fusion(bf16[256,3072]{1,0:T(8,128)(2,1)S(1)} %copy-done.3, bf16[3072,8192]{1,0:T(8,128)(2,1)} %param.16, f32[256,8192]{1,0:T(8,128)} %convolution_add_fusion.1, bf16[256,8192]{1,0:T(8,128)(2,1)} %gather_fusion.2, pred[256]{0:T(512)(128)(4,1)S(1)} %get-tuple-element.6), kind=kOutput, calls=%fused_computation.23 | convolution fusion | flops 12903776256 | bytes 68681984 | tf_op jit(solution)/shard_map/dot_general | solution.py:53
  661.9 58.3 %multiply_reduce_fusion = bf16[256,8]{0,1:T(8,128)(2,1)S(1)} fusion(f32[256,256]{0,1:T(8,128)S(1)} %fusion.27, bf16[256,8192,8]{1,2,0:T(8,128)(2,1)} %param.22, bf16[256,8192]{1,0:T(8,128)(2,1)} %fusion.12), kind=kOutput, calls=%fused_computation.29 | convolution fusion | flops 8590981120 | bytes 38014976 | tf_op jit(solution)/shard_map/tk,akr->tar/dot_general | solution.py:10
  720.4 1.3 scatter_custom_fusion.2
  721.8 22.6 %all_to_all.66 = bf16[128,8,8]{1,2,0:T(8,128)(2,1)S(1)} all-to-all(bf16[128,8,8]{1,2,0:T(8,128)(2,1)S(1)} %copy.34), channel_id=1, replica_groups=mesh['rep'=1,'data'=128] {'data'}, dimensions={0} | all-to-all | bytes 32768 | tf_op jit(solution)/shard_map/all_to_all | solution.py:57
  744.5 0.3 mul.101
  744.8 1.8 fusion.13
  746.6 95.9 %all_to_all.67 = bf16[128,8,3072]{2,1,0:T(8,128)(2,1)} all-to-all(bf16[128,8,3072]{2,1,0:T(8,128)(2,1)S(1)} %fusion.13), channel_id=1, replica_groups=mesh['rep'=1,'data'=128] {'data'}, dimensions={0} | all-to-all | bytes 12582912 | tf_op jit(solution)/shard_map/all_to_all | solution.py:58
  842.6 6.7 gather_fusion
  849.3 23.1 %fusion.16 = bf16[256,3072]{1,0:T(8,128)(2,1)} fusion(bf16[256,8192]{1,0:T(8,128)(2,1)} %fusion.12, bf16[8192,3072]{1,0:T(8,128)(2,1)} %param.17, bf16[256,3072]{1,0:T(8,128)(2,1)S(1)} %copy-done.3, bf16[256,3072]{1,0:T(8,128)(2,1)S(1)} %gather_fusion, pred[256]{0:T(512)(128)(4,1)S(1)} %get-tuple-element.6), kind=kOutput, calls=%fused_computation.28 | convolution fusion | flops 12889620480 | bytes 59244800 | tf_op jit(solution)/shard_map/dot_general | solution.py:59
  (30 shorter events, 1.1 us)
Async XLA Ops:
  0.0 75.9 %copy-start = (bf16[2,8,8192]{2,1,0:T(8,128)(2,1)S(1)}, bf16[2,8,8192]{2,1,0:T(8,128)(2,1)}, u32[]{:S(2)}) copy-start(bf16[2,8,8192]{2,1,0:T(8,128)(2,1)} %param.19) | copy-start | bytes 786436
  3.5 52.3 %all-to-all-start = ((s32[128,8,1]{1,2,0:T(1,128)}), s32[128,8,1]{1,2,0:T(1,128)S(1)}, u32[]{:S(2)}, u32[]{:S(2)}) async-start(s32[128,8,1]{1,2,0:T(1,128)} %bitcast.4), calls=%async_computation | async-start | bytes 131072 | tf_op jit(solution)/shard_map/all_to_all | solution.py:41
  14.7 19.9 %copy-start.3 = (bf16[256,3072]{1,0:T(8,128)(2,1)S(1)}, bf16[256,3072]{1,0:T(8,128)(2,1)}, u32[]{:S(2)}) copy-start(bf16[256,3072]{1,0:T(8,128)(2,1)} %param.13) | copy-start | bytes 4718596
  55.8 19.9 %all-to-all-start.1 = ((bf16[128,8,16]{2,1,0:T(8,128)(2,1)}), bf16[128,8,16]{2,1,0:T(8,128)(2,1)S(1)}, u32[]{:S(2)}, u32[]{:S(2)}) async-start(bf16[128,8,16]{2,1,0:T(8,128)(2,1)} %bitcast.6), calls=%async_computation.1 | async-start | bytes 524288 | tf_op jit(solution)/shard_map/all_to_all | solution.py:46
  84.0 6.4 copy-start.2
  84.0 251.3 %all-to-all-start.2 = ((bf16[128,8,8192]{2,1,0:T(8,128)(2,1)}), bf16[128,8,8192]{2,1,0:T(8,128)(2,1)}, u32[]{:S(2)}, u32[]{:S(2)}) async-start(bf16[128,8,8192]{2,1,0:T(8,128)(2,1)} %fusion.4), calls=%async_computation.2 | async-start | bytes 33554432 | tf_op jit(solution)/shard_map/all_to_all | solution.py:49
  335.3 257.8 %all-to-all-start.3 = ((bf16[128,8,8192]{2,1,0:T(8,128)(2,1)}), bf16[128,8,8192]{2,1,0:T(8,128)(2,1)}, u32[]{:S(2)}, u32[]{:S(2)}) async-start(bf16[128,8,8192]{2,1,0:T(8,128)(2,1)} %fusion.5), calls=%async_computation.3 | async-start | bytes 33554432 | tf_op jit(solution)/shard_map/all_to_all | solution.py:50
  661.9 82.9 %copy-start.4 = (bf16[2,8,3072]{2,1,0:T(8,128)(2,1)S(1)}, bf16[2,8,3072]{2,1,0:T(8,128)(2,1)}, u32[]{:S(2)}) copy-start(bf16[2,8,3072]{2,1,0:T(8,128)(2,1)} %param.23) | copy-start | bytes 294916
  849.3 23.1 %copy-start.1 = (bf16[2,8,8192]{2,1,0:T(8,128)(2,1)S(1)}, bf16[2,8,8192]{2,1,0:T(8,128)(2,1)}, u32[]{:S(2)}) copy-start(bf16[2,8,8192]{2,1,0:T(8,128)(2,1)} %param.19) | copy-start | bytes 786436
where the time goes:
time: 887 us; the launch traced here: 873 us
  waiting for transfers between devices  473 us (53%)
  matrix products  190 us (21%)
  blocking collectives  119 us (13%)
  local copies, waits for them, and re-layouts  48 us (5%)
  starting transfers between devices  39.9 us (4%)
    all_to_all x1, waiting for transfers between devices, device_fn(): back_gate = lax.all_to_all(delta_gate, 'data', 0, 0, tiled=True)  237 us
    all_to_all x1, waiting for transfers between devices, device_fn(): back_up = lax.all_to_all(delta_up, 'data', 0, 0, tiled=True)  228 us
    dot_general x3, matrix products, pick_low(): jnp.einsum('tk,akr->tar', act_rows, a_all, preferred_element_type=jnp.flo...  97.3 us
    all_to_all x1, blocking collectives, device_fn(): lax.all_to_all(value_a7(recv_down, local_hot, b_down), 'data', 0, 0, tile...  95.9 us
    dot_general x1, matrix products, device_fn(): jnp.dot(hidden, w_gate, preferred_element_type=jnp.float32)  26.2 us
    dot_general x1, matrix products, device_fn(): jnp.dot(hidden, w_up, preferred_element_type=jnp.float32)  25.5 us
    dot_general x1, matrix products, device_fn(): jnp.dot(hid_act, w_down, preferred_element_type=jnp.float32)  23.1 us
    all_to_all x1, blocking collectives, device_fn(): recv_down = lax.all_to_all(send_down, 'data', 0, 0, tiled=True)  22.6 us
  transfers between devices with their start and end apart: 4, of which 3 were waited for; matrix products, arithmetic and copies ran while one was open for 8% of the time, Pallas kernels for 0%

commit v1 on v0

v1 whole, which is shorter than its diff:
```python
import jax
import jax.numpy as jnp
from jax import lax
from jax.experimental import pallas as pl
from jax.experimental.pallas import tpu as pltpu
from jax.sharding import PartitionSpec as P

SCALE = 2.0
BF = jnp.bfloat16
F32 = jnp.float32
NT = (((1,), (1,)), ((), ()))
TN = (((0,), (0,)), ((), ()))
TILE = 512
ROWS = 256


def iota(shape, dim):
    return lax.broadcasted_iota(jnp.int32, shape, dim)


def select_rows(rank):
    return jnp.where(iota((16, ROWS), 0) == (iota((16, ROWS), 1) & (rank - 1)), 1.0, 0.0).astype(BF)


def pack_low(low, ids):
    row = iota(low.shape, 0)
    return jnp.where(row < 8, low, jnp.where(row == 8, (ids & 15).astype(F32), jnp.where(row == 9, (ids >> 4).astype(F32), 0.0))).astype(BF)


def spread_low(packet, spread, tokens):
    row, col = iota((16, 384), 0), iota((16, 384), 1)
    pick = jnp.where(col < 128, jnp.where((row < 8) & (row == (col & 7)), 1.0, 0.0),
                     jnp.where(row == jnp.where(col < 256, 8, 9), 1.0, 0.0)).astype(BF)
    wide = lax.dot_general(packet, pick, TN, preferred_element_type=F32)
    lane = (iota((tokens, 128), 1) >> 3).astype(F32)
    mine = jnp.where(wide[:, 128:256] == lane, wide[:, :128], 0.0)
    block = wide[:, 256:]
    for b in range(spread.shape[1] // 128):
        spread[:, b * 128:(b + 1) * 128] = jnp.where(block == float(b), mine, 0.0).astype(BF)


def hidden_kernel(dims, x, ids, ids_up, ag, au, wg, wu, bg, bu, h,
                  wbuf, acc, bsl, snd, rec, spread, low, pk, rpk,
                  w_sem, a_sem, s0_s, s0_r, s1_s, s1_r, s2_s, s2_r, own_sem, p_s, p_r, d_s, d_r, h_sem):
    nx, ny, nz = dims
    nq = 2 * nx
    tokens, width = x.shape
    hidden = wg.shape[1]
    rows = ag.shape[0]
    slab = hidden // nq
    half = slab // 2
    tile = half
    tiles = hidden // tile
    rank = 8
    me = lax.axis_index('data')
    c, px, py, pz = me % 2, (me // 2) % nx, (me // (2 * nx)) % ny, me // (2 * nx * ny)

    def dev(z, y, xx, cc):
        return {'data': ((z * ny + y) * nx + xx) * 2 + cc}

    def at(t, l, m, z, cc):
        return dev(z, m, l, cc) if t == 0 else dev(z, l, m, cc)

    line = [px, py]
    other = [py, px]
    mine = [line[t] * 2 + c for t in range(2)]

    def member(t, q):
        return at(t, q // 2, other[t], pz, q % 2)

    barrier = pltpu.get_barrier_semaphore()
    partners = []
    for t in range(2):
        partners += [member(t, (mine[t] + k) % nq) for k in range(1, nq) if not (t == 1 and k == 0)]
    partners += [dev((pz + k) % nz, py, px, c) for k in range(1, nz)]
    for p in partners:
        pl.semaphore_signal(barrier, inc=1, device_id=p, device_id_type=pl.DeviceIdType.MESH)

    def w_copy(i, t):
        s = (i % 2) * 2 + t
        return pltpu.make_async_copy((wg, wu)[t].at[:, pl.ds(pl.multiple_of(i * tile, 128), tile)], wbuf.at[s], w_sem.at[s])

    chunks = width // tile

    def a_copies(i, t):
        s = (i % 2) * 2 + t
        return [pltpu.make_async_copy((ag, au)[t].at[pl.ds(pl.multiple_of(i * ROWS, ROWS), ROWS), pl.ds(j * tile, tile)],
                                      snd.at[s * chunks + j], a_sem.at[s, j]) for j in range(chunks)]

    for i in range(min(2, rows // ROWS)):
        for t in range(2):
            for cp in a_copies(i, t):
                cp.start()
    for i in range(2):
        for t in range(2):
            w_copy(i, t).start()

    pl.semaphore_wait(barrier, len(partners))

    bsrc = (bg, bu)

    def own(t, hf):
        col = pl.multiple_of(mine[t] * slab + hf * half, 128)
        return pltpu.make_async_copy(bsrc[t].at[:, pl.ds(col, half)],
                                     bsl.at[t, hf, pz, other[t], pl.ds(pl.multiple_of(mine[t] * 16, 16), 16)], own_sem.at[t, hf])

    def stage0(t, hf, k):
        q = (mine[t] + k) % nq
        col = pl.multiple_of(q * slab + hf * half, 128)
        return pltpu.make_async_remote_copy(
            bsrc[t].at[:, pl.ds(col, half)], bsl.at[t, hf, pz, other[t], pl.ds(pl.multiple_of(mine[t] * 16, 16), 16)],
            s0_s.at[t, hf, k], s0_r.at[t, hf, k], device_id=member(t, q), device_id_type=pl.DeviceIdType.MESH)

    def along(t, hf, k):
        if hf == 0:
            n = ny if t == 0 else nx
            return at(t, line[t], (other[t] + k) % n, pz, c)
        return at(t, line[t], other[t], (pz + k) % nz, c)

    def count(t, hf):
        return (ny if t == 0 else nx) if hf == 0 else nz

    def stage1(t, hf, k):
        ref = bsl.at[t, hf, pz, other[t]]
        return pltpu.make_async_remote_copy(ref, ref, s1_s.at[t, hf, k], s1_r.at[t, hf, k],
                                            device_id=along(t, hf, k), device_id_type=pl.DeviceIdType.MESH)

    def stage2(t, hf, k):
        ref = bsl.at[t, hf, pz] if hf == 0 else bsl.at[t, hf, :, other[t]]
        return pltpu.make_async_remote_copy(ref, ref, s2_s.at[t, hf, k], s2_r.at[t, hf, k],
                                            device_id=along(t, 1 - hf, k), device_id_type=pl.DeviceIdType.MESH)

    both = [(t, hf) for t in range(2) for hf in range(2)]
    for t, hf in both:
        own(t, hf).start()
        for k in range(1, nq):
            stage0(t, hf, k).start()

    def low_block(i, _):
        sel = select_rows(rank)
        for t in range(2):
            s = (i % 2) * 2 + t
            total = jnp.zeros((ROWS, tokens), F32)
            for j, cp in enumerate(a_copies(i, t)):
                cp.wait()
                total += lax.dot_general(snd[s * chunks + j], x[:, j * tile:(j + 1) * tile], NT, preferred_element_type=F32)
            adapter = (iota((ROWS, tokens), 0) + i * ROWS) >> 3
            kept = jnp.where(adapter == ids[...], total, 0.0).astype(BF)
            low[t] += jnp.dot(sel, kept, preferred_element_type=F32)

            @pl.when(i + 2 < rows // ROWS)
            def _():
                for cp in a_copies(i + 2, t):
                    cp.start()
        return 0

    low[...] = jnp.zeros_like(low)
    nblk = rows // ROWS
    first = max(1, nblk // 4)
    lax.fori_loop(0, first, low_block, 0)

    for t, hf in both:
        own(t, hf).wait()
        for k in range(1, nq):
            stage0(t, hf, k).wait()
    for t, hf in both:
        for k in range(1, count(t, hf)):
            stage1(t, hf, k).start()

    lax.fori_loop(first, nblk, low_block, 0)

    def packet(t, k):
        return pltpu.make_async_remote_copy(pk.at[t], rpk.at[t, k], p_s.at[t, k], p_r.at[t, k],
                                            device_id=member(t, (mine[t] + k) % nq), device_id_type=pl.DeviceIdType.MESH)

    for t in range(2):
        pk[t] = pack_low(low[t], (ids, ids_up)[t][...])
        for k in range(1, nq):
            packet(t, k).start()

    def base_tile(i, _):
        for t in range(2):
            s = (i % 2) * 2 + t
            w_copy(i, t).wait()
            acc[t, i] = jnp.dot(x[...], wbuf[s], preferred_element_type=F32)

            @pl.when(i + 2 < tiles)
            def _():
                w_copy(i + 2, t).start()
        return 0

    early = tiles // 4
    lax.fori_loop(0, early, base_tile, 0)
    for t, hf in both:
        for k in range(1, count(t, hf)):
            stage1(t, hf, k).wait()
        for k in range(1, count(t, 1 - hf)):
            stage2(t, hf, k).start()
    lax.fori_loop(early, tiles, base_tile, 0)

    for t in range(2):
        for k in range(1, nq):
            packet(t, k).wait()
    for t, hf in both:
        for k in range(1, count(t, 1 - hf)):
            stage2(t, hf, k).wait()

    def back(t, k):
        s = 2 * (t * nq + k)
        return pltpu.make_async_remote_copy(snd.at[pl.ds(s, 2)], rec.at[t, mine[t]], d_s.at[t, k], d_r.at[t, k],
                                            device_id=member(t, (mine[t] + nq - k) % nq), device_id_type=pl.DeviceIdType.MESH)

    for k in range(1, nq + 1):
        for t in range(2):
            kk = k % nq
            if kk:
                spread_low(rpk[t, kk], spread, tokens)
            else:
                spread_low(pk[t], spread, tokens)
            for hf in range(2):
                out = jnp.dot(spread[...], bsl[t, hf].reshape(rows, half), preferred_element_type=F32)
                out = (SCALE * out).astype(BF)
                if kk:
                    snd[2 * (t * nq + kk) + hf] = out
                else:
                    rec[t, mine[t], hf] = out
            if kk:
                back(t, kk).start()

    for k in range(1, nq):
        for t in range(2):
            back(t, k).wait()

    def h_copy(i):
        return pltpu.make_async_copy(rec.at[0, i // 2, i % 2], h.at[:, pl.ds(pl.multiple_of(i * tile, 128), tile)], h_sem.at[i])

    def final(i, _):
        q, hf = i // 2, i % 2
        g = acc[0, i] + rec[0, q, hf].astype(F32)
        u = acc[1, i] + rec[1, q, hf].astype(F32)
        rec[0, q, hf] = (g * jax.nn.sigmoid(g) * u).astype(BF)
        h_copy(i).start()
        return 0

    lax.fori_loop(0, tiles, final, 0)
    lax.fori_loop(0, tiles, lambda i, _: (h_copy(i).wait(), 0)[1], 0)


def hidden_call(dims, x, ids, ids_up, ag, au, wg, wu, bg, bu):
    nx, ny, nz = dims
    nq = 2 * nx
    tokens, width = x.shape
    rows, hidden = ag.shape[0], wg.shape[1]
    half = hidden // nq // 2
    tiles = hidden // half
    dma = pltpu.SemaphoreType.DMA
    vm = pl.BlockSpec(memory_space=pltpu.VMEM)
    anym = pl.BlockSpec(memory_space=pl.ANY)
    n1 = max(nx, ny, nz)
    import functools
    return pl.pallas_call(
        functools.partial(hidden_kernel, dims),
        out_shape=jax.ShapeDtypeStruct((tokens, hidden), BF),
        in_specs=[vm] * 3 + [anym] * 6,
        out_specs=anym,
        scratch_shapes=[
            pltpu.VMEM((4, width, half), BF),
            pltpu.VMEM((2, tiles, tokens, half), F32),
            pltpu.VMEM((2, 2, nz, nx, nx * 32, half), BF),
            pltpu.VMEM((4 * nq, tokens, half), BF),
            pltpu.VMEM((2, nq, 2, tokens, half), BF),
            pltpu.VMEM((tokens, rows), BF),
            pltpu.VMEM((2, 16, tokens), F32),
            pltpu.VMEM((2, 16, tokens), BF),
            pltpu.VMEM((2, nq, 16, tokens), BF),
            dma((4,)), dma((4, width // half)),
            dma((2, 2, nq)), dma((2, 2, nq)), dma((2, 2, n1)), dma((2, 2, n1)), dma((2, 2, n1)), dma((2, 2, n1)),
            dma((2, 2)), dma((2, nq)), dma((2, nq)), dma((2, nq)), dma((2, nq)), dma((tiles,)),
        ],
        compiler_params=pltpu.CompilerParams(collective_id=0, has_side_effects=True, vmem_limit_bytes=67_000_000),
        cost_estimate=pl.CostEstimate(flops=6 * tokens * width * hidden, bytes_accessed=4 * width * hidden, transcendentals=tokens * hidden),
        name='hidden',
    )(x, ids, ids_up, ag, au, wg, wu, bg, bu)


def down_kernel(x, ids, h, ad, bd, wd, out, abuf, wbuf, bbuf, spread, low, a_sem, w_sem, b_sem):
    tokens, width = x.shape
    hidden = h.shape[1]
    rows = ad.shape[0]
    nblk = rows // ROWS
    tile = min(TILE, width)
    kt = hidden // 2
    steps = width // tile

    def a_copy(i):
        return pltpu.make_async_copy(ad.at[pl.ds(pl.multiple_of(i * ROWS, ROWS), ROWS)], abuf.at[i % 3], a_sem.at[i % 3])

    def w_copy(i, k):
        s = (i % 2) * 2 + k
        return pltpu.make_async_copy(wd.at[pl.ds(k * kt, kt), pl.ds(pl.multiple_of(i * tile, 128), tile)], wbuf.at[s], w_sem.at[s])

    def b_copy(i):
        return pltpu.make_async_copy(bd.at[:, pl.ds(pl.multiple_of(i * tile, 128), tile)], bbuf.at[i % 2], b_sem.at[i % 2])

    for i in range(min(3, nblk)):
        a_copy(i).start()
    for i in range(min(2, steps)):
        b_copy(i).start()
        for k in range(2):
            w_copy(i, k).start()
    low[...] = jnp.zeros_like(low)

    def low_block(i, _):
        a_copy(i).wait()
        total = lax.dot_general(abuf[i % 3], h[...], NT, preferred_element_type=F32)
        adapter = (iota((ROWS, tokens), 0) + i * ROWS) >> 3
        kept = jnp.where(adapter == ids[...], total, 0.0).astype(BF)
        low[...] += jnp.dot(select_rows(8), kept, preferred_element_type=F32)

        @pl.when(i + 3 < nblk)
        def _():
            a_copy(i + 3).start()
        return 0

    lax.fori_loop(0, nblk, low_block, 0)
    spread_low(pack_low(low[...], ids[...]), spread, tokens)

    def step(i, _):
        b_copy(i).wait()
        delta = (SCALE * jnp.dot(spread[...], bbuf[i % 2], preferred_element_type=F32)).astype(BF).astype(F32)
        w_copy(i, 0).wait()
        y = jnp.dot(h[:, :kt], wbuf[(i % 2) * 2], preferred_element_type=F32)
        w_copy(i, 1).wait()
        y += jnp.dot(h[:, kt:], wbuf[(i % 2) * 2 + 1], preferred_element_type=F32)
        cols = pl.ds(pl.multiple_of(i * tile, 128), tile)
        out[:, cols] = (x[:, cols].astype(F32) + (y + delta)).astype(BF)

        @pl.when(i + 2 < steps)
        def _():
            b_copy(i + 2).start()
            w_copy(i + 2, 0).start()
            w_copy(i + 2, 1).start()
        return 0

    lax.fori_loop(0, steps, step, 0)


def down_call(x, ids, h, ad, bd, wd):
    tokens, width = x.shape
    rows, hidden = ad.shape
    tile = min(TILE, width)
    dma = pltpu.SemaphoreType.DMA
    vm = pl.BlockSpec(memory_space=pltpu.VMEM)
    anym = pl.BlockSpec(memory_space=pl.ANY)
    return pl.pallas_call(
        down_kernel,
        out_shape=jax.ShapeDtypeStruct((tokens, width), BF),
        in_specs=[vm] * 3 + [anym] * 3,
        out_specs=vm,
        scratch_shapes=[
            pltpu.VMEM((3, ROWS, hidden), BF),
            pltpu.VMEM((4, hidden // 2, tile), BF),
            pltpu.VMEM((2, rows, tile), BF),
            pltpu.VMEM((tokens, rows), BF),
            pltpu.VMEM((16, tokens), F32),
            dma((3,)), dma((4,)), dma((2,)),
        ],
        compiler_params=pltpu.CompilerParams(vmem_limit_bytes=67_000_000),
        cost_estimate=pl.CostEstimate(flops=2 * tokens * width * hidden, bytes_accessed=4 * width * hidden, transcendentals=0),
        name='down',
    )(x, ids, h, ad, bd, wd)


def solution(mesh, dims=(4, 4, 4)):
    row_spec = P(('rep', 'data'), None)
    tok_spec = P(('rep', 'data'))
    two = P(None, None)
    three = P(None, None, None)
    owned = P('data', None, None)
    nx, ny, nz = dims

    def device_fn(x, ids, wg, wu, wd, ag, bg, au, bu, ad, bd):
        own, r, f = bg.shape
        adapters = ag.shape[0]
        flat = lambda a: jnp.transpose(a, (0, 2, 1)).reshape(adapters * r, a.shape[1])
        b_down = lax.all_gather(bd.reshape(own * r, bd.shape[2]), 'data', axis=0, tiled=True)
        lx, ly, w = 2 * own, 2 * own * nx, nx
        rest, xs, ys = ids % lx, (ids // lx) % nx, (ids // ly) % ny
        zs = ids // (ly * ny)
        ids_up = ((zs * nx + xs) * ny + ys) * lx + rest
        ids1 = ids.reshape(1, -1)
        h = hidden_call(dims, x, ids1, ids_up.reshape(1, -1), flat(ag), flat(au), wg, wu, bg.reshape(own * r, f), bu.reshape(own * r, f))
        return down_call(x, ids1, h, flat(ad), b_down, wd)

    return jax.shard_map(device_fn, mesh=mesh, in_specs=(row_spec, tok_spec, two, two, two, three, owned, three, owned, three, owned), out_specs=row_spec, check_vma=False)
```

time: 887 us -> 223 us (0.25)
  the two profiles are of different devices: /device:TPU:2 before, /device:TPU:0 now
where the time goes in v1:
time: 223 us
  Pallas kernels  208 us (93%)
  between operations  13.4 us (6%)
    pallas_call x1, Pallas kernels, hidden_call(): pl.pallas_call(functools.partial(hidden_kernel, dims), out_shape=jax.Shap...  163 us
    pallas_call x1, Pallas kernels, down_call(): pl.pallas_call(down_kernel, out_shape=jax.ShapeDtypeStruct((tokens, width...  44.2 us
  transfers between devices with their start and end apart: 1, of which 0 were waited for; matrix products, arithmetic and copies ran while one was open for 1% of the time, Pallas kernels for 73%

profile of v1, /device:TPU:0, one launch (start us, length us, event | category | flops | bytes accessed | tf_op | source)
XLA Modules:
  0.0 223.0 jit_solution(14673291380698239320)
XLA Ops:
  6.5 0.0 all-gather.2.cloned.1.call-start
  6.5 0.7 all-gather.2.cloned.1.call-update
  7.3 1.3 fusion.2
  8.5 163.4 %hidden.1.h = bf16[256,8192]{1,0:T(8,128)(2,1)} custom-call(bf16[256,3072]{1,0:T(8,128)(2,1)} %x.3, s32[1,256]{1,0:T(1,128)} %bitcast.16, s32[1,256]{1,0:T(1,128)} %bitcast.18, bf16[2048,3072]{1,0:T(8,128)(2,1)} %bitcast.19, bf16[2048,3072]{1,0:T(8,128)(2,1)} %bitcast.20, bf16[3072,8192]{1,0:T(8,128)(2,1)} %wg.1, bf16[3072,8192]{1,0:T(8,128)(2,1)} %wu.1, ...), custom_call_target="tpu_custom_call" | custom-call | flops 38654705664 | bytes 100663296 | tf_op jit(solution)/shard_map/hidden/pallas_call | solution.py:261
  171.9 0.0 all-gather.2.cloned.1.call-done.bd
  172.0 44.2 %down.1 = bf16[256,3072]{1,0:T(8,128)(2,1)} custom-call(bf16[256,3072]{1,0:T(8,128)(2,1)} %x.3, s32[1,256]{1,0:T(1,128)} %bitcast.17, bf16[256,8192]{1,0:T(8,128)(2,1)} %hidden.1.h, bf16[2048,8192]{1,0:T(8,128)(2,1)} %bitcast.14, bf16[2048,3072]{1,0:T(8,128)(2,1)} %all-gather.2.cloned.1.call-done.bd, bf16[8192,3072]{1,0:T(8,128)(2,1)} %wd.1), custom_call_target="tpu_custom_call" | custom-call | flops 12884901888 | bytes 100663296 | tf_op jit(solution)/shard_map/down/pallas_call | solution.py:355
Async XLA Ops:
  6.5 165.4 %all-gather.2.cloned.1.call-start = ((), (), s32[]{:S(2)}) async-start(), calls=%async_computation | async-start | bytes 12681216 | tf_op jit(solution)/shard_map/all_gather | solution.py:386
Sparse Core Ops, SparseCore 0:
  10.4 107.2 all-gather.1

commit v2 on v1

v2 whole, which is shorter than its diff:
```python
import functools

import jax
import jax.numpy as jnp
from jax import lax
from jax.experimental import pallas as pl
from jax.experimental.pallas import tpu as pltpu
from jax.sharding import PartitionSpec as P

SCALE = 2.0
BF = jnp.bfloat16
F32 = jnp.float32
NT = (((1,), (1,)), ((), ()))
TN = (((0,), (0,)), ((), ()))
TILE = 512
ROWS = 256


def iota(shape, dim):
    return lax.broadcasted_iota(jnp.int32, shape, dim)


def select_rows(rank):
    return jnp.where(iota((16, ROWS), 0) == (iota((16, ROWS), 1) & (rank - 1)), 1.0, 0.0).astype(BF)


def pack_low(low, ids):
    row = iota(low.shape, 0)
    return jnp.where(row < 8, low, jnp.where(row == 8, (ids & 15).astype(F32), jnp.where(row == 9, (ids >> 4).astype(F32), 0.0))).astype(BF)


def spread_low(packet, spread, tokens):
    row, col = iota((16, 384), 0), iota((16, 384), 1)
    pick = jnp.where(col < 128, jnp.where((row < 8) & (row == (col & 7)), 1.0, 0.0),
                     jnp.where(row == jnp.where(col < 256, 8, 9), 1.0, 0.0)).astype(BF)
    wide = lax.dot_general(packet, pick, TN, preferred_element_type=F32)
    lane = (iota((tokens, 128), 1) >> 3).astype(F32)
    mine = jnp.where(wide[:, 128:256] == lane, wide[:, :128], 0.0)
    block = wide[:, 256:]
    for b in range(spread.shape[1] // 128):
        spread[:, b * 128:(b + 1) * 128] = jnp.where(block == float(b), mine, 0.0).astype(BF)


def hidden_kernel(dims, x, ids, ids_up, ag, au, wg, wu, bg, bu, ad, wd, y, pkd,
                  wbuf, acc, b0, b1, snd, rec, spread, low, adn, pk, rpk,
                  w_sem, a_sem, s0_s, s0_r, s1_s, s1_r, s2_s, s2_r, own_sem, p_s, p_r, d_s, d_r):
    nx, ny, nz = dims
    nq = 2 * nx
    tokens, width = x.shape
    hidden = wg.shape[1]
    rows = ag.shape[0]
    slab = hidden // nq
    tile = slab // 2
    tiles = hidden // tile
    cut = b0.shape[-1]
    bsl = (b0, b1)
    spans = (pl.ds(0, cut), pl.ds(cut, slab - cut))
    me = lax.axis_index('data')
    c, px, py, pz = me % 2, (me // 2) % nx, (me // (2 * nx)) % ny, me // (2 * nx * ny)
    mesh_id = pl.DeviceIdType.MESH

    def dev(z, yy, xx, cc):
        return {'data': ((z * ny + yy) * nx + xx) * 2 + cc}

    def at(t, l, m, z, cc):
        return dev(z, m, l, cc) if t == 0 else dev(z, l, m, cc)

    line = [px, py]
    other = [py, px]
    mine = [line[t] * 2 + c for t in range(2)]

    def member(t, q):
        return at(t, q // 2, other[t], pz, q % 2)

    barrier = pltpu.get_barrier_semaphore()
    partners = []
    for t in range(2):
        partners += [member(t, (mine[t] + k) % nq) for k in range(1, nq)]
    partners += [dev((pz + k) % nz, py, px, c) for k in range(1, nz)]
    for p in partners:
        pl.semaphore_signal(barrier, inc=1, device_id=p, device_id_type=mesh_id)

    chunks = width // tile

    def w_copies(i, t):
        s = (i % 2) * 2 + t
        cols = pl.ds(pl.multiple_of(i * tile, 128), tile)
        return [pltpu.make_async_copy((wg, wu)[t].at[pl.ds(j * tile, tile), cols], wbuf.at[s, j], w_sem.at[s, j]) for j in range(chunks)]

    def tile_at(n):
        return 2 * ((2 * (px + py) + c + n // 2) % nq) + n % 2

    def d_copies(n, t):
        s = (n % 2) * 2 + t
        i = tile_at(n)
        span = pl.ds(pl.multiple_of(i * tile, 128), tile)
        if t == 0:
            return [pltpu.make_async_copy(ad.at[pl.ds(j * tile, tile), span], wbuf.at[s, j], w_sem.at[s, j]) for j in range(rows // tile)]
        return [pltpu.make_async_copy(wd.at[span, pl.ds(j * tile, tile)], wbuf.at[s, j], w_sem.at[s, j]) for j in range(chunks)]

    wide = width // slab

    def a_copies(i, t):
        s = (i % 2) * 2 + t
        return [pltpu.make_async_copy((ag, au)[t].at[pl.ds(pl.multiple_of(i * ROWS, ROWS), ROWS), pl.ds(j * slab, slab)],
                                      snd.at[s * wide + j], a_sem.at[s, j]) for j in range(wide)]

    def start(copies):
        for cp in copies:
            cp.start()

    def wait(copies):
        for cp in copies:
            cp.wait()

    for i in range(min(2, rows // ROWS)):
        for t in range(2):
            start(a_copies(i, t))
    for i in range(2):
        for t in range(2):
            start(w_copies(i, t))

    pl.semaphore_wait(barrier, len(partners))

    bsrc = (bg, bu)
    widths = (cut, slab - cut)

    def own_rows(t, hf):
        return bsl[hf].at[t, pz, other[t], pl.ds(pl.multiple_of(mine[t] * 16, 16), 16)]

    def source(t, hf, q):
        return bsrc[t].at[:, pl.ds(pl.multiple_of(q * slab + hf * cut, 128), widths[hf])]

    def own(t, hf):
        return pltpu.make_async_copy(source(t, hf, mine[t]), own_rows(t, hf), own_sem.at[t, hf])

    def stage0(t, hf, k):
        q = (mine[t] + k) % nq
        return pltpu.make_async_remote_copy(source(t, hf, q), own_rows(t, hf), s0_s.at[t, hf, k], s0_r.at[t, hf, k],
                                            device_id=member(t, q), device_id_type=mesh_id)

    def count(t, hf):
        return (ny if t == 0 else nx) if hf == 0 else nz

    def along(t, hf, k):
        if hf == 0:
            return at(t, line[t], (other[t] + k) % count(t, 0), pz, c)
        return at(t, line[t], other[t], (pz + k) % nz, c)

    def block(t, hf, b):
        if hf == 0:
            return bsl[0].at[t, pz, (other[t] + b) % count(t, 0)]
        return bsl[1].at[t, (pz + b) % nz, other[t]]

    def stage1(t, hf, k):
        ref = block(t, hf, 0)
        return pltpu.make_async_remote_copy(ref, ref, s1_s.at[t, hf, k], s1_r.at[t, hf, k],
                                            device_id=along(t, hf, k), device_id_type=mesh_id)

    def stage2(t, hf, k, b):
        ref = block(t, hf, b)
        return pltpu.make_async_remote_copy(ref, ref, s2_s.at[t, hf, k, b], s2_r.at[t, hf, k, b],
                                            device_id=along(t, 1 - hf, k), device_id_type=mesh_id)

    both = [(t, hf) for hf in (1, 0) for t in range(2)]
    for t, hf in both:
        own(t, hf).start()
        for k in range(1, nq):
            stage0(t, hf, k).start()

    nblk = rows // ROWS

    def low_block(i, _):
        sel = select_rows(8)
        for t in range(2):
            s = (i % 2) * 2 + t
            total = jnp.zeros((ROWS, tokens), F32)
            for j, cp in enumerate(a_copies(i, t)):
                cp.wait()
                total += lax.dot_general(snd[s * wide + j], x[:, j * slab:(j + 1) * slab], NT, preferred_element_type=F32)
            adapter = (iota((ROWS, tokens), 0) + i * ROWS) >> 3
            kept = jnp.where(adapter == ids[...], total, 0.0).astype(BF)
            low[t] += jnp.dot(sel, kept, preferred_element_type=F32)

            @pl.when(i + 2 < nblk)
            def _():
                start(a_copies(i + 2, t))
        return 0

    low[...] = jnp.zeros_like(low)
    first = max(1, nblk // 4)
    lax.fori_loop(0, first, low_block, 0)

    for t, hf in both:
        own(t, hf).wait()
        wait([stage0(t, hf, k) for k in range(1, nq)])
        start([stage1(t, hf, k) for k in range(1, count(t, hf))])
    for t, hf in both:
        start([stage2(t, hf, k, 0) for k in range(1, count(t, 1 - hf))])

    lax.fori_loop(first, nblk, low_block, 0)

    def packet(t, k):
        return pltpu.make_async_remote_copy(pk.at[t], rpk.at[t, mine[t]], p_s.at[t, k], p_r.at[t, k],
                                            device_id=member(t, (mine[t] + k) % nq), device_id_type=mesh_id)

    for t in range(2):
        pk[t] = pack_low(low[t], (ids, ids_up)[t][...])
        rpk[t, mine[t]] = pk[t]
        for k in range(1, nq):
            packet(t, k).start()

    def relay(t, hf):
        n = count(t, hf)
        for k in range(1, n):
            stage1(t, hf, k).wait()
            start([stage2(t, hf, kk, n - k) for kk in range(1, count(t, 1 - hf))])

    for t in range(2):
        relay(t, 0)

    def base_tile(i, _):
        for t in range(2):
            s = (i % 2) * 2 + t
            wait(w_copies(i, t))
            acc[t, i] = jnp.dot(x[...], wbuf[s, :chunks].reshape(width, tile), preferred_element_type=F32)

            @pl.when(i + 2 < tiles)
            def _():
                start(w_copies(i + 2, t))

            @pl.when(i + 2 >= tiles)
            def _():
                start(d_copies(i + 2 - tiles, t))
        return 0

    early = tiles // 8
    lax.fori_loop(0, early, base_tile, 0)
    for t in range(2):
        relay(t, 1)
    lax.fori_loop(early, tiles, base_tile, 0)

    for t in range(2):
        for k in range(1, nq):
            packet(t, k).wait()
    for t, hf in both:
        for k in range(1, count(t, 1 - hf)):
            for b in range(count(t, hf)):
                stage2(t, hf, k, b).wait()

    def back(t, k, d):
        return pltpu.make_async_remote_copy(snd.at[t * nq + k], rec.at[t, mine[t]], d_s.at[t, k], d_r.at[t, k],
                                            device_id=member(t, d), device_id_type=mesh_id)

    def target(t, k):
        return (mine[t] + 4 * nq - 2 * other[t] - k) % nq

    def delta_step(k, _):
        for t in range(2):
            d = target(t, k)
            spread_low(rpk[t, d], spread, tokens)
            for hf in range(2):
                out = jnp.dot(spread[...], bsl[hf][t].reshape(rows, widths[hf]), preferred_element_type=F32)
                snd[t * nq + k, :, spans[hf]] = (SCALE * out).astype(BF)

            @pl.when(d == mine[t])
            def _():
                rec[t, mine[t]] = snd[t * nq + k]

            @pl.when(d != mine[t])
            def _():
                back(t, k, d).start()
        return 0

    lax.fori_loop(0, nq, delta_step, 0)

    y[...] = jnp.zeros_like(y)
    adn[...] = jnp.zeros_like(adn)

    def final(k, _):
        q = (2 * (px + py) + c + k) % nq
        for t in range(2):
            @pl.when(q != mine[t])
            def _():
                pltpu.make_async_remote_copy(snd.at[t * nq + k], rec.at[t, q], d_s.at[t, k], d_r.at[t, k],
                                             device_id=member(t, target(t, k)), device_id_type=mesh_id).wait_recv()
        for hf in range(2):
            n = 2 * k + hf
            cols = pl.ds(hf * tile, tile)
            g = acc[0, 2 * q + hf] + rec[0, q, :, cols].astype(F32)
            u = acc[1, 2 * q + hf] + rec[1, q, :, cols].astype(F32)
            h = (g * jax.nn.sigmoid(g) * u).astype(BF)
            wait(d_copies(n, 0))
            for j in range(rows // tile):
                span = pl.ds(j * tile, tile)
                adn[span] += lax.dot_general(wbuf[2 * hf, j], h, NT, preferred_element_type=F32)
            wait(d_copies(n, 1))
            for j in range(chunks):
                span = pl.ds(j * tile, tile)
                y[:, span] += jnp.dot(h, wbuf[2 * hf + 1, j], preferred_element_type=F32)

            @pl.when(n + 2 < tiles)
            def _():
                for t in range(2):
                    start(d_copies(n + 2, t))
        return 0

    lax.fori_loop(0, nq, final, 0)

    low[0] = jnp.zeros_like(low[0])

    def down_block(i, _):
        adapter = (iota((ROWS, tokens), 0) + i * ROWS) >> 3
        kept = jnp.where(adapter == ids[...], adn[pl.ds(pl.multiple_of(i * ROWS, ROWS), ROWS)], 0.0).astype(BF)
        low[0] += jnp.dot(select_rows(8), kept, preferred_element_type=F32)
        return 0

    lax.fori_loop(0, nblk, down_block, 0)
    pkd[...] = pack_low(low[0], ids[...])

    def sent(k, _):
        for t in range(2):
            d = target(t, k)

            @pl.when(d != mine[t])
            def _():
                back(t, k, d).wait_send()
        return 0

    lax.fori_loop(0, nq, sent, 0)


def hidden_call(dims, x, ids, ids_up, ag, au, wg, wu, bg, bu, ad, wd):
    nx, ny, nz = dims
    nq = 2 * nx
    tokens, width = x.shape
    rows, hidden = ag.shape[0], wg.shape[1]
    slab = hidden // nq
    tile = slab // 2
    cut = max(128, slab // 4)
    tiles = hidden // tile
    dma = pltpu.SemaphoreType.DMA
    vm = pl.BlockSpec(memory_space=pltpu.VMEM)
    anym = pl.BlockSpec(memory_space=pl.ANY)
    n1 = max(nx, ny, nz)
    nch = max(width, rows) // tile
    return pl.pallas_call(
        functools.partial(hidden_kernel, dims),
        out_shape=[jax.ShapeDtypeStruct((tokens, width), F32), jax.ShapeDtypeStruct((16, tokens), BF)],
        in_specs=[vm] * 3 + [anym] * 8,
        out_specs=[vm, vm],
        scratch_shapes=[
            pltpu.VMEM((4, nch, tile, tile), BF),
            pltpu.VMEM((2, tiles, tokens, tile), F32),
            pltpu.VMEM((2, nz, nx, nx * 32, cut), BF),
            pltpu.VMEM((2, nz, nx, nx * 32, slab - cut), BF),
            pltpu.VMEM((2 * nq, tokens, slab), BF),
            pltpu.VMEM((2, nq, tokens, slab), BF),
            pltpu.VMEM((tokens, rows), BF),
            pltpu.VMEM((2, 16, tokens), F32),
            pltpu.VMEM((rows, tokens), F32),
            pltpu.VMEM((2, 16, tokens), BF),
            pltpu.VMEM((2, nq, 16, tokens), BF),
            dma((4, nch)), dma((4, width // slab)),
            dma((2, 2, nq)), dma((2, 2, nq)), dma((2, 2, n1)), dma((2, 2, n1)), dma((2, 2, n1, n1)), dma((2, 2, n1, n1)),
            dma((2, 2)), dma((2, nq)), dma((2, nq)), dma((2, nq)), dma((2, nq)),
        ],
        compiler_params=pltpu.CompilerParams(collective_id=0, has_side_effects=True, vmem_limit_bytes=67_000_000),
        cost_estimate=pl.CostEstimate(flops=6 * tokens * width * hidden, bytes_accessed=6 * width * hidden, transcendentals=tokens * hidden),
        name='hidden',
    )(x, ids, ids_up, ag, au, wg, wu, bg, bu, ad, wd)


def down_kernel(x, y, packet, bd, out, spread):
    @pl.when(pl.program_id(0) == 0)
    def _():
        spread_low(packet[...], spread, x.shape[0])

    delta = (SCALE * jnp.dot(spread[...], bd[...], preferred_element_type=F32)).astype(BF).astype(F32)
    out[...] = (x[...].astype(F32) + (y[...] + delta)).astype(BF)


def down_call(x, y, packet, bd):
    tokens, width = x.shape
    rows = bd.shape[0]
    tile = min(TILE, width)
    rowblk = pl.BlockSpec((tokens, tile), lambda i: (0, i))
    return pl.pallas_call(
        down_kernel,
        grid=(width // tile,),
        out_shape=jax.ShapeDtypeStruct((tokens, width), BF),
        in_specs=[rowblk, rowblk, pl.BlockSpec((16, tokens), lambda i: (0, 0)), pl.BlockSpec((rows, tile), lambda i: (0, i))],
        out_specs=rowblk,
        scratch_shapes=[pltpu.VMEM((tokens, rows), BF)],
        cost_estimate=pl.CostEstimate(flops=2 * tokens * width * rows, bytes_accessed=2 * width * rows, transcendentals=0),
        name='down',
    )(x, y, packet, bd)


def solution(mesh, dims=(4, 4, 4)):
    row_spec = P(('rep', 'data'), None)
    tok_spec = P(('rep', 'data'))
    two = P(None, None)
    three = P(None, None, None)
    owned = P('data', None, None)
    nx, ny, nz = dims

    def device_fn(x, ids, wg, wu, wd, ag, bg, au, bu, ad, bd):
        own, r, f = bg.shape
        adapters = ag.shape[0]
        flat = lambda a: jnp.transpose(a, (0, 2, 1)).reshape(adapters * r, a.shape[1])
        b_down = lax.all_gather(bd.reshape(own * r, bd.shape[2]), 'data', axis=0, tiled=True)
        lx, ly = 2 * own, 2 * own * nx
        rest, xs, ys = ids % lx, (ids // lx) % nx, (ids // ly) % ny
        zs = ids // (ly * ny)
        ids_up = ((zs * nx + xs) * ny + ys) * lx + rest
        ids1 = ids.reshape(1, -1)
        y, packet = hidden_call(dims, x, ids1, ids_up.reshape(1, -1), flat(ag), flat(au), wg, wu, bg.reshape(own * r, f), bu.reshape(own * r, f), flat(ad), wd)
        return down_call(x, y, packet, b_down)

    return jax.shard_map(device_fn, mesh=mesh, in_specs=(row_spec, tok_spec, two, two, two, three, owned, three, owned, three, owned), out_specs=row_spec, check_vma=False)
```

time: 223 us -> 188 us (0.84)
  the two profiles are of different devices: /device:TPU:0 before, /device:TPU:6 now
where the time goes in v2:
time: 188 us; the launch traced here: 187 us
  Pallas kernels  172 us (91%)
  between operations  13.4 us (7%)
    pallas_call x1, Pallas kernels, hidden_call(): pl.pallas_call(functools.partial(hidden_kernel, dims), out_shape=[jax.Sha...  161 us
    pallas_call x1, Pallas kernels, down_call(): pl.pallas_call(down_kernel, grid=(width // tile,), out_shape=jax.ShapeDty...  10.5 us
  transfers between devices with their start and end apart: 1, of which 0 were waited for; matrix products, arithmetic and copies ran while one was open for 1% of the time, Pallas kernels for 86%

profile of v2, /device:TPU:6, one launch (start us, length us, event | category | flops | bytes accessed | tf_op | source)
XLA Modules:
  0.0 187.4 jit_solution(7759179895000882861)
XLA Ops:
  6.5 0.0 all-gather.2.cloned.1.call-start
  6.5 0.7 all-gather.2.cloned.1.call-update
  7.3 1.3 fusion.2
  8.5 161.5 %hidden.1 = (f32[256,3072]{1,0:T(8,128)}, bf16[16,256]{1,0:T(8,128)(2,1)}) custom-call(bf16[256,3072]{1,0:T(8,128)(2,1)} %x.3, s32[1,256]{1,0:T(1,128)} %bitcast.20, s32[1,256]{1,0:T(1,128)} %bitcast.21, bf16[2048,3072]{1,0:T(8,128)(2,1)} %bitcast.15, bf16[2048,3072]{1,0:T(8,128)(2,1)} %bitcast.16, bf16[3072,8192]{1,0:T(8,128)(2,1)} %wg.1, ...), custom_call_target="tpu_custom_call" | custom-call | flops 38654705664 | bytes 150994944 | tf_op jit(solution)/shard_map/hidden/pallas_call | solution.py:347
  170.0 0.0 all-gather.2.cloned.1.call-done.bd
  170.0 10.5 %down.1 = bf16[256,3072]{1,0:T(8,128)(2,1)} custom-call(bf16[256,3072]{1,0:T(8,128)(2,1)} %x.3, f32[256,3072]{1,0:T(8,128)} %get-tuple-element.7.y, bf16[16,256]{1,0:T(8,128)(2,1)} %get-tuple-element.8.packet, bf16[2048,3072]{1,0:T(8,128)(2,1)} %all-gather.2.cloned.1.call-done.bd), custom_call_target="tpu_custom_call" | custom-call | flops 3221225472 | bytes 12582912 | tf_op jit(solution)/shard_map/down/pallas_call | solution.py:388
Async XLA Ops:
  6.5 163.5 %all-gather.2.cloned.1.call-start = ((), (), s32[]{:S(2)}) async-start(), calls=%async_computation | async-start | bytes 12681216 | tf_op jit(solution)/shard_map/all_gather | solution.py:412
Sparse Core Ops, SparseCore 0:
  10.4 125.5 all-gather.1

commit v3 on v2

--- a/solution.py
+++ b/solution.py
@@ -12,7 +12,6 @@
 F32 = jnp.float32
 NT = (((1,), (1,)), ((), ()))
 TN = (((0,), (0,)), ((), ()))
-TILE = 512
 ROWS = 256
 
 
@@ -41,9 +40,13 @@
         spread[:, b * 128:(b + 1) * 128] = jnp.where(block == float(b), mine, 0.0).astype(BF)
 
 
-def hidden_kernel(dims, x, ids, ids_up, ag, au, wg, wu, bg, bu, ad, wd, y, pkd,
-                  wbuf, acc, b0, b1, snd, rec, spread, low, adn, pk, rpk,
-                  w_sem, a_sem, s0_s, s0_r, s1_s, s1_r, s2_s, s2_r, own_sem, p_s, p_r, d_s, d_r):
+def layer_kernel(dims, x, ids, ag, au, wg, wu, bg, bu, ad, wd, bd, out,
+                 wbuf, acc, b0, b1, b2, b3, snd, rec, spread, low, adn, y, pk, rpk,
+                  w_sem, a_sem, s0_s, s0_r, s1_s, s1_r, s2_s, s2_r, own_sem, p_s, p_r, d_s, d_r, o_sem):
+    bits = [n.bit_length() - 1 for n in (2 * (bg.shape[0] // 8), dims[0], dims[1])]
+    low_mask, xs = ids[...] & ((1 << bits[0]) - 1), (ids[...] >> bits[0]) & (dims[0] - 1)
+    ys, zs = (ids[...] >> (bits[0] + bits[1])) & (dims[1] - 1), ids[...] >> sum(bits)
+    ids_up = (((zs * dims[0] + xs) * dims[1] + ys) << bits[0]) + low_mask
     nx, ny, nz = dims
     nq = 2 * nx
     tokens, width = x.shape
@@ -53,7 +56,6 @@
     tile = slab // 2
     tiles = hidden // tile
     cut = b0.shape[-1]
-    bsl = (b0, b1)
     spans = (pl.ds(0, cut), pl.ds(cut, slab - cut))
     me = lax.axis_index('data')
     c, px, py, pz = me % 2, (me // 2) % nx, (me // (2 * nx)) % ny, me // (2 * nx * ny)
@@ -63,11 +65,11 @@
         return {'data': ((z * ny + yy) * nx + xx) * 2 + cc}
 
     def at(t, l, m, z, cc):
-        return dev(z, m, l, cc) if t == 0 else dev(z, l, m, cc)
-
-    line = [px, py]
-    other = [py, px]
-    mine = [line[t] * 2 + c for t in range(2)]
+        return dev(z, m, l, cc) if t % 2 == 0 else dev(z, l, m, cc)
+
+    line = [px, py, px, py]
+    other = [py, px, py, px]
+    mine = [line[t] * 2 + c for t in range(4)]
 
     def member(t, q):
         return at(t, q // 2, other[t], pz, q % 2)
@@ -122,25 +124,31 @@
 
     pl.semaphore_wait(barrier, len(partners))
 
-    bsrc = (bg, bu)
+    w2, w3 = b2.shape[-1], b3.shape[-1]
+    slots = {(0, 0): 0, (0, 1): 1, (1, 0): 2, (1, 1): 3, (2, 0): 4, (3, 0): 5}
     widths = (cut, slab - cut)
 
+    def held(t, hf):
+        return (b0, b1)[hf].at[t] if t < 2 else (b2, b3)[t - 2]
+
     def own_rows(t, hf):
-        return bsl[hf].at[t, pz, other[t], pl.ds(pl.multiple_of(mine[t] * 16, 16), 16)]
+        return held(t, hf).at[pz, other[t], pl.ds(pl.multiple_of(mine[t] * 16, 16), 16)]
 
     def source(t, hf, q):
-        return bsrc[t].at[:, pl.ds(pl.multiple_of(q * slab + hf * cut, 128), widths[hf])]
+        if t < 2:
+            return (bg, bu)[t].at[:, pl.ds(pl.multiple_of(q * slab + hf * cut, 128), widths[hf])]
+        return bd.at[:, pl.ds(pl.multiple_of(q * w2 if t == 2 else nq * w2 + q * w3, 128), w2 if t == 2 else w3)]
 
     def own(t, hf):
-        return pltpu.make_async_copy(source(t, hf, mine[t]), own_rows(t, hf), own_sem.at[t, hf])
+        return pltpu.make_async_copy(source(t, hf, mine[t]), own_rows(t, hf), own_sem.at[slots[t, hf]])
 
     def stage0(t, hf, k):
-        q = (mine[t] + k) % nq
-        return pltpu.make_async_remote_copy(source(t, hf, q), own_rows(t, hf), s0_s.at[t, hf, k], s0_r.at[t, hf, k],
+        q, g = (mine[t] + k) % nq, slots[t, hf]
+        return pltpu.make_async_remote_copy(source(t, hf, q), own_rows(t, hf), s0_s.at[g, k], s0_r.at[g, k],
                                             device_id=member(t, q), device_id_type=mesh_id)
 
     def count(t, hf):
-        return (ny if t == 0 else nx) if hf == 0 else nz
+        return (ny if t % 2 == 0 else nx) if hf == 0 else nz
 
     def along(t, hf, k):
         if hf == 0:
@@ -149,21 +157,22 @@
 
     def block(t, hf, b):
         if hf == 0:
-            return bsl[0].at[t, pz, (other[t] + b) % count(t, 0)]
-        return bsl[1].at[t, (pz + b) % nz, other[t]]
+            return held(t, hf).at[pz, (other[t] + b) % count(t, 0)]
+        return held(t, hf).at[(pz + b) % nz, other[t]]
 
     def stage1(t, hf, k):
         ref = block(t, hf, 0)
-        return pltpu.make_async_remote_copy(ref, ref, s1_s.at[t, hf, k], s1_r.at[t, hf, k],
+        return pltpu.make_async_remote_copy(ref, ref, s1_s.at[slots[t, hf], k], s1_r.at[slots[t, hf], k],
                                             device_id=along(t, hf, k), device_id_type=mesh_id)
 
     def stage2(t, hf, k, b):
         ref = block(t, hf, b)
-        return pltpu.make_async_remote_copy(ref, ref, s2_s.at[t, hf, k, b], s2_r.at[t, hf, k, b],
+        return pltpu.make_async_remote_copy(ref, ref, s2_s.at[slots[t, hf], k, b], s2_r.at[slots[t, hf], k, b],
                                             device_id=along(t, 1 - hf, k), device_id_type=mesh_id)
 
     both = [(t, hf) for hf in (1, 0) for t in range(2)]
-    for t, hf in both:
+    downs = [(2, 0), (3, 0)]
+    for t, hf in both + downs:
         own(t, hf).start()
         for k in range(1, nq):
             stage0(t, hf, k).start()
@@ -199,16 +208,23 @@
         start([stage2(t, hf, k, 0) for k in range(1, count(t, 1 - hf))])
 
     lax.fori_loop(first, nblk, low_block, 0)
+    for t, hf in downs:
+        own(t, hf).wait()
+        wait([stage0(t, hf, k) for k in range(1, nq)])
+        start([stage1(t, hf, k) for k in range(1, count(t, hf))])
 
     def packet(t, k):
         return pltpu.make_async_remote_copy(pk.at[t], rpk.at[t, mine[t]], p_s.at[t, k], p_r.at[t, k],
                                             device_id=member(t, (mine[t] + k) % nq), device_id_type=mesh_id)
 
-    for t in range(2):
-        pk[t] = pack_low(low[t], (ids, ids_up)[t][...])
+    def send_packet(t, rows_in):
+        pk[t] = pack_low(rows_in, ids[...] if t % 2 == 0 else ids_up)
         rpk[t, mine[t]] = pk[t]
         for k in range(1, nq):
             packet(t, k).start()
+
+    for t in range(2):
+        send_packet(t, low[t])
 
     def relay(t, hf):
         n = count(t, hf)
@@ -239,6 +255,11 @@
     for t in range(2):
         relay(t, 1)
     lax.fori_loop(early, tiles, base_tile, 0)
+    for t, hf in downs:
+        for k in range(1, count(t, hf)):
+            stage1(t, hf, k).wait()
+        for b in range(count(t, hf)):
+            start([stage2(t, hf, k, b) for k in range(1, nz)])
 
     for t in range(2):
         for k in range(1, nq):
@@ -260,7 +281,7 @@
             d = target(t, k)
             spread_low(rpk[t, d], spread, tokens)
             for hf in range(2):
-                out = jnp.dot(spread[...], bsl[hf][t].reshape(rows, widths[hf]), preferred_element_type=F32)
+                out = jnp.dot(spread[...], (b0, b1)[hf][t].reshape(rows, widths[hf]), preferred_element_type=F32)
                 snd[t * nq + k, :, spans[hf]] = (SCALE * out).astype(BF)
 
             @pl.when(d == mine[t])
@@ -316,7 +337,8 @@
         return 0
 
     lax.fori_loop(0, nblk, down_block, 0)
-    pkd[...] = pack_low(low[0], ids[...])
+    for t in (2, 3):
+        send_packet(t, low[0])
 
     def sent(k, _):
         for t in range(2):
@@ -328,9 +350,73 @@
         return 0
 
     lax.fori_loop(0, nq, sent, 0)
-
-
-def hidden_call(dims, x, ids, ids_up, ag, au, wg, wu, bg, bu, ad, wd):
+    for t, hf in downs:
+        for k in range(1, nz):
+            for b in range(count(t, hf)):
+                stage2(t, hf, k, b).wait()
+        for k in range(1, nq):
+            packet(t, k).wait()
+
+    def down_back(t, k, q, d):
+        w = pl.ds(0, w2 if t == 2 else w3)
+        return pltpu.make_async_remote_copy(snd.at[(t - 2) * nq + k, :, w], rec.at[t - 2, q, :, w], d_s.at[t, k], d_r.at[t, k],
+                                            device_id=member(t, d), device_id_type=mesh_id)
+
+    def down_step(k, _):
+        for t in (2, 3):
+            d = target(t, k)
+            w = pl.ds(0, w2 if t == 2 else w3)
+            spread_low(rpk[t, d], spread, tokens)
+            delta = jnp.dot(spread[...], held(t, 0)[...].reshape(rows, w2 if t == 2 else w3), preferred_element_type=F32)
+            delta = (SCALE * delta).astype(BF)
+            snd[(t - 2) * nq + k, :, w] = delta
+
+            @pl.when(d == mine[t])
+            def _():
+                rec[t - 2, mine[t], :, w] = snd[(t - 2) * nq + k, :, w]
+
+            @pl.when(d != mine[t])
+            def _():
+                down_back(t, k, mine[t], d).start()
+        return 0
+
+    lax.fori_loop(0, nq, down_step, 0)
+
+    def out_copy(t, q):
+        w = w2 if t == 2 else w3
+        cols = pl.ds(pl.multiple_of(q * w2 if t == 2 else nq * w2 + q * w3, 128), w)
+        return pltpu.make_async_copy(rec.at[t - 2, q, :, pl.ds(0, w)], out.at[:, cols], o_sem.at[t - 2, q])
+
+    def finish(k, _):
+        q = (2 * (px + py) + c + k) % nq
+        for t in (2, 3):
+            @pl.when(q != mine[t])
+            def _():
+                down_back(t, k, q, target(t, k)).wait_recv()
+            w = w2 if t == 2 else w3
+            cols = pl.ds(pl.multiple_of(q * w2 if t == 2 else nq * w2 + q * w3, 128), w)
+            part = pl.ds(0, w)
+            rec[t - 2, q, :, part] = (x[:, cols].astype(F32) + (y[:, cols] + rec[t - 2, q, :, part].astype(F32))).astype(BF)
+            out_copy(t, q).start()
+        return 0
+
+    lax.fori_loop(0, nq, finish, 0)
+
+    def down_sent(k, _):
+        for t in (2, 3):
+            d = target(t, k)
+
+            @pl.when(d != mine[t])
+            def _():
+                down_back(t, k, mine[t], d).wait_send()
+
+            out_copy(t, k).wait()
+        return 0
+
+    lax.fori_loop(0, nq, down_sent, 0)
+
+
+def layer_call(dims, x, ids, ag, au, wg, wu, bg, bu, ad, wd, bd):
     nx, ny, nz = dims
     nq = 2 * nx
     tokens, width = x.shape
@@ -338,63 +424,43 @@
     slab = hidden // nq
     tile = slab // 2
     cut = max(128, slab // 4)
+    w2 = width // (3 * nq) * 2
+    w3 = width // (3 * nq)
     tiles = hidden // tile
     dma = pltpu.SemaphoreType.DMA
     vm = pl.BlockSpec(memory_space=pltpu.VMEM)
     anym = pl.BlockSpec(memory_space=pl.ANY)
     n1 = max(nx, ny, nz)
     nch = max(width, rows) // tile
+    wide = width // slab
     return pl.pallas_call(
-        functools.partial(hidden_kernel, dims),
-        out_shape=[jax.ShapeDtypeStruct((tokens, width), F32), jax.ShapeDtypeStruct((16, tokens), BF)],
-        in_specs=[vm] * 3 + [anym] * 8,
-        out_specs=[vm, vm],
+        functools.partial(layer_kernel, dims),
+        out_shape=jax.ShapeDtypeStruct((tokens, width), BF),
+        in_specs=[vm] * 2 + [anym] * 9,
+        out_specs=anym,
         scratch_shapes=[
             pltpu.VMEM((4, nch, tile, tile), BF),
             pltpu.VMEM((2, tiles, tokens, tile), F32),
             pltpu.VMEM((2, nz, nx, nx * 32, cut), BF),
             pltpu.VMEM((2, nz, nx, nx * 32, slab - cut), BF),
-            pltpu.VMEM((2 * nq, tokens, slab), BF),
+            pltpu.VMEM((nz, nx, nx * 32, w2), BF),
+            pltpu.VMEM((nz, nx, nx * 32, w3), BF),
+            pltpu.VMEM((max(2 * nq, 4 * wide), tokens, slab), BF),
             pltpu.VMEM((2, nq, tokens, slab), BF),
             pltpu.VMEM((tokens, rows), BF),
             pltpu.VMEM((2, 16, tokens), F32),
             pltpu.VMEM((rows, tokens), F32),
-            pltpu.VMEM((2, 16, tokens), BF),
-            pltpu.VMEM((2, nq, 16, tokens), BF),
-            dma((4, nch)), dma((4, width // slab)),
-            dma((2, 2, nq)), dma((2, 2, nq)), dma((2, 2, n1)), dma((2, 2, n1)), dma((2, 2, n1, n1)), dma((2, 2, n1, n1)),
-            dma((2, 2)), dma((2, nq)), dma((2, nq)), dma((2, nq)), dma((2, nq)),
+            pltpu.VMEM((tokens, width), F32),
+            pltpu.VMEM((4, 16, tokens), BF),
+            pltpu.VMEM((4, nq, 16, tokens), BF),
+            dma((4, nch)), dma((4, wide)),
+            dma((6, nq)), dma((6, nq)), dma((6, n1)), dma((6, n1)), dma((6, n1, n1)), dma((6, n1, n1)),
+            dma((6,)), dma((4, nq)), dma((4, nq)), dma((4, nq)), dma((4, nq)), dma((2, nq)),
         ],
         compiler_params=pltpu.CompilerParams(collective_id=0, has_side_effects=True, vmem_limit_bytes=67_000_000),
         cost_estimate=pl.CostEstimate(flops=6 * tokens * width * hidden, bytes_accessed=6 * width * hidden, transcendentals=tokens * hidden),
-        name='hidden',
-    )(x, ids, ids_up, ag, au, wg, wu, bg, bu, ad, wd)
-
-
-def down_kernel(x, y, packet, bd, out, spread):
-    @pl.when(pl.program_id(0) == 0)
-    def _():
-        spread_low(packet[...], spread, x.shape[0])
-
-    delta = (SCALE * jnp.dot(spread[...], bd[...], preferred_element_type=F32)).astype(BF).astype(F32)
-    out[...] = (x[...].astype(F32) + (y[...] + delta)).astype(BF)
-
-
-def down_call(x, y, packet, bd):
-    tokens, width = x.shape
-    rows = bd.shape[0]
-    tile = min(TILE, width)
-    rowblk = pl.BlockSpec((tokens, tile), lambda i: (0, i))
-    return pl.pallas_call(
-        down_kernel,
-        grid=(width // tile,),
-        out_shape=jax.ShapeDtypeStruct((tokens, width), BF),
-        in_specs=[rowblk, rowblk, pl.BlockSpec((16, tokens), lambda i: (0, 0)), pl.BlockSpec((rows, tile), lambda i: (0, i))],
-        out_specs=rowblk,
-        scratch_shapes=[pltpu.VMEM((tokens, rows), BF)],
-        cost_estimate=pl.CostEstimate(flops=2 * tokens * width * rows, bytes_accessed=2 * width * rows, transcendentals=0),
-        name='down',
-    )(x, y, packet, bd)
+        name='layer',
+    )(x, ids, ag, au, wg, wu, bg, bu, ad, wd, bd)
 
 
 def solution(mesh, dims=(4, 4, 4)):
@@ -403,19 +469,12 @@
     two = P(None, None)
     three = P(None, None, None)
     owned = P('data', None, None)
-    nx, ny, nz = dims
 
     def device_fn(x, ids, wg, wu, wd, ag, bg, au, bu, ad, bd):
-        own, r, f = bg.shape
+        own, r = bg.shape[:2]
         adapters = ag.shape[0]
         flat = lambda a: jnp.transpose(a, (0, 2, 1)).reshape(adapters * r, a.shape[1])
-        b_down = lax.all_gather(bd.reshape(own * r, bd.shape[2]), 'data', axis=0, tiled=True)
-        lx, ly = 2 * own, 2 * own * nx
-        rest, xs, ys = ids % lx, (ids // lx) % nx, (ids // ly) % ny
-        zs = ids // (ly * ny)
-        ids_up = ((zs * nx + xs) * ny + ys) * lx + rest
-        ids1 = ids.reshape(1, -1)
-        y, packet = hidden_call(dims, x, ids1, ids_up.reshape(1, -1), flat(ag), flat(au), wg, wu, bg.reshape(own * r, f), bu.reshape(own * r, f), flat(ad), wd)
-        return down_call(x, y, packet, b_down)
+        rows = lambda a: a.reshape(own * r, a.shape[2])
+        return layer_call(dims, x, ids.reshape(1, -1), flat(ag), flat(au), wg, wu, rows(bg), rows(bu), flat(ad), wd, rows(bd))
 
     return jax.shard_map(device_fn, mesh=mesh, in_specs=(row_spec, tok_spec, two, two, two, three, owned, three, owned, three, owned), out_specs=row_spec, check_vma=False)

time: 188 us -> 168 us (0.89)
  the two profiles are of different devices: /device:TPU:6 before, /device:TPU:0 now
where the time goes in v3:
time: 168 us
  Pallas kernels  165 us (98%)
  local copies, waits for them, and re-layouts  2.65 us (2%)
    pallas_call x1, Pallas kernels, layer_call(): pl.pallas_call(functools.partial(layer_kernel, dims), out_shape=jax.Shape...  165 us

profile of v3, /device:TPU:0, one launch (start us, length us, event | category | flops | bytes accessed | tf_op | source)
XLA Modules:
  0.0 167.8 jit_solution(8370153490188105354)
XLA Ops:
  0.0 165.2 %layer.1 = bf16[256,3072]{1,0:T(8,128)(2,1)} custom-call(bf16[256,3072]{1,0:T(8,128)(2,1)} %x.1, s32[1,256]{1,0:T(1,128)} %bitcast.19, bf16[2048,3072]{1,0:T(8,128)(2,1)} %bitcast.14, bf16[2048,3072]{1,0:T(8,128)(2,1)} %bitcast.15, bf16[3072,8192]{1,0:T(8,128)(2,1)} %wg.1, bf16[3072,8192]{1,0:T(8,128)(2,1)} %wu.1, bf16[16,8192]{1,0:T(8,128)(2,1)} %bitcast.16, ...), custom_call_target="tpu_custom_call" | custom-call | flops 38654705664 | bytes 150994944 | tf_op jit(solution)/shard_map/layer/pallas_call | solution.py:436
  165.2 2.7 %copy.13 = bf16[256,3072]{1,0:T(8,128)(2,1)} copy(bf16[256,3072]{1,0:T(8,128)(2,1)} %layer.1) | data formatting | bytes 3145728

commit v4 on v3

--- a/solution.py
+++ b/solution.py
@@ -10,7 +10,6 @@
 SCALE = 2.0
 BF = jnp.bfloat16
 F32 = jnp.float32
-NT = (((1,), (1,)), ((), ()))
 TN = (((0,), (0,)), ((), ()))
 ROWS = 256
 
@@ -178,15 +177,22 @@
             stage0(t, hf, k).start()
 
     nblk = rows // ROWS
+    per = slab // tokens
+
+    def x_turned(j):
+        return snd.at[4 * wide + j // per, :, pl.ds(j % per * tokens, tokens)]
+
+    for j in range(width // tokens):
+        x_turned(j)[...] = x[:, j * tokens:(j + 1) * tokens].T
 
     def low_block(i, _):
         sel = select_rows(8)
         for t in range(2):
             s = (i % 2) * 2 + t
+            wait(a_copies(i, t))
             total = jnp.zeros((ROWS, tokens), F32)
-            for j, cp in enumerate(a_copies(i, t)):
-                cp.wait()
-                total += lax.dot_general(snd[s * wide + j], x[:, j * slab:(j + 1) * slab], NT, preferred_element_type=F32)
+            for j in range(width // tokens):
+                total += jnp.dot(snd[s * wide + j // per, :, pl.ds(j % per * tokens, tokens)], x_turned(j)[...], preferred_element_type=F32)
             adapter = (iota((ROWS, tokens), 0) + i * ROWS) >> 3
             kept = jnp.where(adapter == ids[...], total, 0.0).astype(BF)
             low[t] += jnp.dot(sel, kept, preferred_element_type=F32)
@@ -276,57 +282,73 @@
     def target(t, k):
         return (mine[t] + 4 * nq - 2 * other[t] - k) % nq
 
-    def delta_step(k, _):
-        for t in range(2):
-            d = target(t, k)
-            spread_low(rpk[t, d], spread, tokens)
+    def delta_step(k):
+        aims = [target(t, k) for t in range(2)]
+        for t in range(2):
+            spread_low(rpk[t, aims[t]], spread.at[t], tokens)
             for hf in range(2):
-                out = jnp.dot(spread[...], (b0, b1)[hf][t].reshape(rows, widths[hf]), preferred_element_type=F32)
-                snd[t * nq + k, :, spans[hf]] = (SCALE * out).astype(BF)
-
-            @pl.when(d == mine[t])
+                out_part = jnp.dot(spread[t], (b0, b1)[hf][t].reshape(rows, widths[hf]), preferred_element_type=F32)
+                snd[t * nq + k, :, spans[hf]] = (SCALE * out_part).astype(BF)
+        for t in range(2):
+            @pl.when(aims[t] == mine[t])
             def _():
                 rec[t, mine[t]] = snd[t * nq + k]
 
-            @pl.when(d != mine[t])
-            def _():
-                back(t, k, d).start()
-        return 0
-
-    lax.fori_loop(0, nq, delta_step, 0)
-
-    y[...] = jnp.zeros_like(y)
-    adn[...] = jnp.zeros_like(adn)
-
-    def final(k, _):
+            @pl.when(aims[t] != mine[t])
+            def _():
+                back(t, k, aims[t]).start()
+
+    def final(k):
         q = (2 * (px + py) + c + k) % nq
         for t in range(2):
             @pl.when(q != mine[t])
             def _():
                 pltpu.make_async_remote_copy(snd.at[t * nq + k], rec.at[t, q], d_s.at[t, k], d_r.at[t, k],
                                              device_id=member(t, target(t, k)), device_id_type=mesh_id).wait_recv()
-        for hf in range(2):
-            n = 2 * k + hf
+
+        def gated(hf):
             cols = pl.ds(hf * tile, tile)
             g = acc[0, 2 * q + hf] + rec[0, q, :, cols].astype(F32)
             u = acc[1, 2 * q + hf] + rec[1, q, :, cols].astype(F32)
-            h = (g * jax.nn.sigmoid(g) * u).astype(BF)
+            rec[0, q, :, cols] = (g * jax.nn.sigmoid(g) * u).astype(BF)
+
+        for hf in range(2):
+            n = 2 * k + hf
             wait(d_copies(n, 0))
+            wait(d_copies(n, 1))
+            if hf == 0:
+                gated(0)
+            h = rec[0, q, :, pl.ds(hf * tile, tile)]
+            turned = h.T
             for j in range(rows // tile):
                 span = pl.ds(j * tile, tile)
-                adn[span] += lax.dot_general(wbuf[2 * hf, j], h, NT, preferred_element_type=F32)
-            wait(d_copies(n, 1))
+                adn[span] += jnp.dot(wbuf[2 * hf, j], turned, preferred_element_type=F32)
             for j in range(chunks):
                 span = pl.ds(j * tile, tile)
                 y[:, span] += jnp.dot(h, wbuf[2 * hf + 1, j], preferred_element_type=F32)
+            if hf == 0:
+                gated(1)
 
             @pl.when(n + 2 < tiles)
             def _():
                 for t in range(2):
                     start(d_copies(n + 2, t))
-        return 0
-
-    lax.fori_loop(0, nq, final, 0)
+
+    y[...] = jnp.zeros_like(y)
+    adn[...] = jnp.zeros_like(adn)
+    lag = nq
+
+    def middle(k, _):
+        @pl.when(k < nq)
+        def _():
+            delta_step(k)
+
+        @pl.when(k >= lag)
+        def _():
+            final(k - lag)
+        return 0
+
+    lax.fori_loop(0, nq + lag, middle, 0)
 
     low[0] = jnp.zeros_like(low[0])
 
@@ -363,21 +385,20 @@
                                             device_id=member(t, d), device_id_type=mesh_id)
 
     def down_step(k, _):
-        for t in (2, 3):
-            d = target(t, k)
-            w = pl.ds(0, w2 if t == 2 else w3)
-            spread_low(rpk[t, d], spread, tokens)
-            delta = jnp.dot(spread[...], held(t, 0)[...].reshape(rows, w2 if t == 2 else w3), preferred_element_type=F32)
-            delta = (SCALE * delta).astype(BF)
-            snd[(t - 2) * nq + k, :, w] = delta
-
-            @pl.when(d == mine[t])
-            def _():
-                rec[t - 2, mine[t], :, w] = snd[(t - 2) * nq + k, :, w]
-
-            @pl.when(d != mine[t])
-            def _():
-                down_back(t, k, mine[t], d).start()
+        aims = [target(t, k) for t in (2, 3)]
+        parts = [pl.ds(0, w2), pl.ds(0, w3)]
+        for i in range(2):
+            spread_low(rpk[i + 2, aims[i]], spread.at[i], tokens)
+            delta = jnp.dot(spread[i], (b2, b3)[i][...].reshape(rows, (w2, w3)[i]), preferred_element_type=F32)
+            snd[i * nq + k, :, parts[i]] = (SCALE * delta).astype(BF)
+        for i in range(2):
+            @pl.when(aims[i] == mine[i + 2])
+            def _():
+                rec[i, mine[i + 2], :, parts[i]] = snd[i * nq + k, :, parts[i]]
+
+            @pl.when(aims[i] != mine[i + 2])
+            def _():
+                down_back(i + 2, k, mine[i + 2], aims[i]).start()
         return 0
 
     lax.fori_loop(0, nq, down_step, 0)
@@ -445,9 +466,9 @@
             pltpu.VMEM((2, nz, nx, nx * 32, slab - cut), BF),
             pltpu.VMEM((nz, nx, nx * 32, w2), BF),
             pltpu.VMEM((nz, nx, nx * 32, w3), BF),
-            pltpu.VMEM((max(2 * nq, 4 * wide), tokens, slab), BF),
+            pltpu.VMEM((max(2 * nq, 5 * wide), tokens, slab), BF),
             pltpu.VMEM((2, nq, tokens, slab), BF),
-            pltpu.VMEM((tokens, rows), BF),
+            pltpu.VMEM((2, tokens, rows), BF),
             pltpu.VMEM((2, 16, tokens), F32),
             pltpu.VMEM((rows, tokens), F32),
             pltpu.VMEM((tokens, width), F32),

time: 168 us -> 167 us (level)
  no operation moved by 1% of the time
where the time goes in v4:
time: 167 us
  Pallas kernels  165 us (99%)
  local copies, waits for them, and re-layouts  2.65 us (2%)
    pallas_call x1, Pallas kernels, layer_call(): pl.pallas_call(functools.partial(layer_kernel, dims), out_shape=jax.Shape...  165 us

profile of v4, /device:TPU:0, one launch (start us, length us, event | category | flops | bytes accessed | tf_op | source)
XLA Modules:
  0.0 167.2 jit_solution(1695611312490845102)
XLA Ops:
  0.0 164.5 %layer.1 = bf16[256,3072]{1,0:T(8,128)(2,1)} custom-call(bf16[256,3072]{1,0:T(8,128)(2,1)} %x.1, s32[1,256]{1,0:T(1,128)} %bitcast.19, bf16[2048,3072]{1,0:T(8,128)(2,1)} %bitcast.14, bf16[2048,3072]{1,0:T(8,128)(2,1)} %bitcast.15, bf16[3072,8192]{1,0:T(8,128)(2,1)} %wg.1, bf16[3072,8192]{1,0:T(8,128)(2,1)} %wu.1, bf16[16,8192]{1,0:T(8,128)(2,1)} %bitcast.16, ...), custom_call_target="tpu_custom_call" | custom-call | flops 38654705664 | bytes 150994944 | tf_op jit(solution)/shard_map/layer/pallas_call | solution.py:457
  164.5 2.7 %copy.13 = bf16[256,3072]{1,0:T(8,128)(2,1)} copy(bf16[256,3072]{1,0:T(8,128)(2,1)} %layer.1) | data formatting | bytes 3145728

commit v5 on v4

--- a/solution.py
+++ b/solution.py
@@ -88,8 +88,21 @@
         cols = pl.ds(pl.multiple_of(i * tile, 128), tile)
         return [pltpu.make_async_copy((wg, wu)[t].at[pl.ds(j * tile, tile), cols], wbuf.at[s, j], w_sem.at[s, j]) for j in range(chunks)]
 
+    def slab_at(k):
+        i = k % nx
+        hop = 3 * ((i + 1) // 2) - i if nx == 4 else i
+        return (px + hop) % nx * 2 + (c + k // nx) % 2
+
     def tile_at(n):
-        return 2 * ((2 * (px + py) + c + n // 2) % nq) + n % 2
+        return 2 * slab_at(n // 2) + n % 2
+
+    def target(t, k):
+        far = nx - 1
+        last = k // (2 * far)
+        r = k % far
+        hop = (1 - last) * (2 - r + 3 * (r // 2) if nx == 4 else 1)
+        flip = (1 - last) * (k // far) + last * (nq - 1 - k)
+        return (line[t] + nx - hop) % nx * 2 + (c + flip) % 2
 
     def d_copies(n, t):
         s = (n % 2) * 2 + t
@@ -105,6 +118,9 @@
         s = (i % 2) * 2 + t
         return [pltpu.make_async_copy((ag, au)[t].at[pl.ds(pl.multiple_of(i * ROWS, ROWS), ROWS), pl.ds(j * slab, slab)],
                                       snd.at[s * wide + j], a_sem.at[s, j]) for j in range(wide)]
+
+    def order(n):
+        return [2, 1, 3] if n == 4 else list(range(1, n))
 
     def start(copies):
         for cp in copies:
@@ -209,15 +225,15 @@
     for t, hf in both:
         own(t, hf).wait()
         wait([stage0(t, hf, k) for k in range(1, nq)])
-        start([stage1(t, hf, k) for k in range(1, count(t, hf))])
+        start([stage1(t, hf, k) for k in order(count(t, hf))])
     for t, hf in both:
-        start([stage2(t, hf, k, 0) for k in range(1, count(t, 1 - hf))])
+        start([stage2(t, hf, k, 0) for k in order(count(t, 1 - hf))])
 
     lax.fori_loop(first, nblk, low_block, 0)
     for t, hf in downs:
         own(t, hf).wait()
         wait([stage0(t, hf, k) for k in range(1, nq)])
-        start([stage1(t, hf, k) for k in range(1, count(t, hf))])
+        start([stage1(t, hf, k) for k in order(count(t, hf))])
 
     def packet(t, k):
         return pltpu.make_async_remote_copy(pk.at[t], rpk.at[t, mine[t]], p_s.at[t, k], p_r.at[t, k],
@@ -236,7 +252,7 @@
         n = count(t, hf)
         for k in range(1, n):
             stage1(t, hf, k).wait()
-            start([stage2(t, hf, kk, n - k) for kk in range(1, count(t, 1 - hf))])
+            start([stage2(t, hf, kk, n - k) for kk in order(count(t, 1 - hf))])
 
     for t in range(2):
         relay(t, 0)
@@ -265,7 +281,7 @@
         for k in range(1, count(t, hf)):
             stage1(t, hf, k).wait()
         for b in range(count(t, hf)):
-            start([stage2(t, hf, k, b) for k in range(1, nz)])
+            start([stage2(t, hf, k, b) for k in order(nz)])
 
     for t in range(2):
         for k in range(1, nq):
@@ -276,11 +292,8 @@
                 stage2(t, hf, k, b).wait()
 
     def back(t, k, d):
-        return pltpu.make_async_remote_copy(snd.at[t * nq + k], rec.at[t, mine[t]], d_s.at[t, k], d_r.at[t, k],
+        return pltpu.make_async_remote_copy(snd.at[t * nq + k], rec.at[t, mine[t]], d_s.at[t, k], d_r.at[t, mine[t]],
                                             device_id=member(t, d), device_id_type=mesh_id)
-
-    def target(t, k):
-        return (mine[t] + 4 * nq - 2 * other[t] - k) % nq
 
     def delta_step(k):
         aims = [target(t, k) for t in range(2)]
@@ -290,21 +303,21 @@
                 out_part = jnp.dot(spread[t], (b0, b1)[hf][t].reshape(rows, widths[hf]), preferred_element_type=F32)
                 snd[t * nq + k, :, spans[hf]] = (SCALE * out_part).astype(BF)
         for t in range(2):
-            @pl.when(aims[t] == mine[t])
+            @pl.when(k == nq - 1)
             def _():
                 rec[t, mine[t]] = snd[t * nq + k]
 
-            @pl.when(aims[t] != mine[t])
+            @pl.when(k < nq - 1)
             def _():
                 back(t, k, aims[t]).start()
 
     def final(k):
-        q = (2 * (px + py) + c + k) % nq
+        q = slab_at(k)
         for t in range(2):
             @pl.when(q != mine[t])
             def _():
-                pltpu.make_async_remote_copy(snd.at[t * nq + k], rec.at[t, q], d_s.at[t, k], d_r.at[t, k],
-                                             device_id=member(t, target(t, k)), device_id_type=mesh_id).wait_recv()
+                pltpu.make_async_remote_copy(snd.at[t * nq + k], rec.at[t, q], d_s.at[t, k], d_r.at[t, q],
+                                             device_id=member(t, q), device_id_type=mesh_id).wait_recv()
 
         def gated(hf):
             cols = pl.ds(hf * tile, tile)
@@ -366,7 +379,7 @@
         for t in range(2):
             d = target(t, k)
 
-            @pl.when(d != mine[t])
+            @pl.when(k < nq - 1)
             def _():
                 back(t, k, d).wait_send()
         return 0
@@ -381,7 +394,7 @@
 
     def down_back(t, k, q, d):
         w = pl.ds(0, w2 if t == 2 else w3)
-        return pltpu.make_async_remote_copy(snd.at[(t - 2) * nq + k, :, w], rec.at[t - 2, q, :, w], d_s.at[t, k], d_r.at[t, k],
+        return pltpu.make_async_remote_copy(snd.at[(t - 2) * nq + k, :, w], rec.at[t - 2, q, :, w], d_s.at[t, k], d_r.at[t, q],
                                             device_id=member(t, d), device_id_type=mesh_id)
 
     def down_step(k, _):
@@ -392,11 +405,11 @@
             delta = jnp.dot(spread[i], (b2, b3)[i][...].reshape(rows, (w2, w3)[i]), preferred_element_type=F32)
             snd[i * nq + k, :, parts[i]] = (SCALE * delta).astype(BF)
         for i in range(2):
-            @pl.when(aims[i] == mine[i + 2])
+            @pl.when(k == nq - 1)
             def _():
                 rec[i, mine[i + 2], :, parts[i]] = snd[i * nq + k, :, parts[i]]
 
-            @pl.when(aims[i] != mine[i + 2])
+            @pl.when(k < nq - 1)
             def _():
                 down_back(i + 2, k, mine[i + 2], aims[i]).start()
         return 0
@@ -409,11 +422,11 @@
         return pltpu.make_async_copy(rec.at[t - 2, q, :, pl.ds(0, w)], out.at[:, cols], o_sem.at[t - 2, q])
 
     def finish(k, _):
-        q = (2 * (px + py) + c + k) % nq
+        q = slab_at(k)
         for t in (2, 3):
             @pl.when(q != mine[t])
             def _():
-                down_back(t, k, q, target(t, k)).wait_recv()
+                down_back(t, k, q, q).wait_recv()
             w = w2 if t == 2 else w3
             cols = pl.ds(pl.multiple_of(q * w2 if t == 2 else nq * w2 + q * w3, 128), w)
             part = pl.ds(0, w)
@@ -427,7 +440,7 @@
         for t in (2, 3):
             d = target(t, k)
 
-            @pl.when(d != mine[t])
+            @pl.when(k < nq - 1)
             def _():
                 down_back(t, k, mine[t], d).wait_send()
 

time: 167 us -> 157 us (0.940)
  Pallas kernels: 165 us -> 153 us
    pallas_call x1, Pallas kernels: 165 us -> 153 us  [layer_call(): pl.pallas_call(functools.partial(layer_kernel, dims), out_shape=jax.Shape...]
where the time goes in v5:
time: 157 us; the launch traced here: 156 us
  Pallas kernels  153 us (97%)
  local copies, waits for them, and re-layouts  2.65 us (2%)
    pallas_call x1, Pallas kernels, layer_call(): pl.pallas_call(functools.partial(layer_kernel, dims), out_shape=jax.Shape...  153 us

profile of v5, /device:TPU:0, one launch (start us, length us, event | category | flops | bytes accessed | tf_op | source)
XLA Modules:
  0.0 155.9 jit_solution(12862934487647514727)
XLA Ops:
  0.0 153.3 %layer.1 = bf16[256,3072]{1,0:T(8,128)(2,1)} custom-call(bf16[256,3072]{1,0:T(8,128)(2,1)} %x.1, s32[1,256]{1,0:T(1,128)} %bitcast.19, bf16[2048,3072]{1,0:T(8,128)(2,1)} %bitcast.14, bf16[2048,3072]{1,0:T(8,128)(2,1)} %bitcast.15, bf16[3072,8192]{1,0:T(8,128)(2,1)} %wg.1, bf16[3072,8192]{1,0:T(8,128)(2,1)} %wu.1, bf16[16,8192]{1,0:T(8,128)(2,1)} %bitcast.16, ...), custom_call_target="tpu_custom_call" | custom-call | flops 38654705664 | bytes 150994944 | tf_op jit(solution)/shard_map/layer/pallas_call | solution.py:470
  153.3 2.7 %copy.13 = bf16[256,3072]{1,0:T(8,128)(2,1)} copy(bf16[256,3072]{1,0:T(8,128)(2,1)} %layer.1) | data formatting | bytes 3145728
